TPU v7x, 128 devices: a whole 4x4x4 slice. The times are simulated.
128 devices in a mesh: section: 4 (over y), wide: 8 (over z, x_hi), narrow: 4 (over x_lo, core).
Axes of the slice: x: 4 (x_hi: 2, x_lo: 2; x = x_hi * 2 + x_lo), y: 4, z: 4, core: 2. Of those that a mesh axis runs over, the one named last changes fastest.
Arguments:
- normed_inputs: bfloat16 [4, 4, 4, 768, 4096], P('section', 'narrow', None, 'wide'), may hold values from -160 to 160
- value_cotangent: bfloat16 [4, 4, 4, 768, 1024], P('section', 'narrow', None, 'wide'), may hold values from -6 to 6
- expert_hidden: bfloat16 [4, 4, 4, 256, 7168], P('section', 'narrow', None, None, 'wide'), may hold values from -40 to 40
- expert_cotangent: bfloat16 [4, 4, 4, 256, 4096], P('section', 'narrow', None, 'wide'), may hold values from -110 to 110
- slot_gate: bfloat16 [4, 4, 4, 256], P('section', 'narrow', None, 'wide'), may hold values from 0.25 to 1
- slot_count: int32 [4, 4, 4], P('section', 'narrow'), may hold values from 129 to 256, as said below
- expert_weight: bfloat16 [4, 7168, 4096], P('section', 'wide', 'narrow'), may hold values from -0.0625 to 0.0625
- expert_moment: float32 [4, 7168, 4096], P('section', 'wide', 'narrow'), may hold values from -6 to 6
- value_weight: bfloat16 [4, 4096, 1024], P('section', ('wide', 'narrow')), may hold values from -0.09375 to 0.09375
- value_moment: float32 [4, 4096, 1024], P('section', ('wide', 'narrow')), may hold values from -6 to 6
Outputs:
- expert_weight_next: bfloat16 [4, 7168, 4096], P('section', 'wide', 'narrow')
- expert_moment_next: float32 [4, 7168, 4096], P('section', 'wide', 'narrow')
- value_weight_next: bfloat16 [4, 4096, 1024], P('section', ('wide', 'narrow'))
- value_moment_next: float32 [4, 4096, 1024], P('section', ('wide', 'narrow'))
Inputs may be any that keep to these rules, and one draw needn't show every extreme that they name: The live slots of a micro-batch are slots 0 to slot_count - 1; in every layer and replica some micro-batch fills all 256 slots.
All inputs are finite; a program needn't handle non-finite values.
Results may differ from a plain program's by a relative error of at most 0.014.
Values may be sent and summed in bfloat16 or wider, within the bound.
A program may use at most 128 MiB of HBM per device.

v0:
```python
import math
import jax
import jax.numpy as jnp
from jax import lax
from jax.sharding import Mesh
from jax.sharding import PartitionSpec as P

D = 4096
FF = 7168
KV = 1024
WIDE = ("wide_0", "wide_1")
NARROW = ("narrow_0", "narrow_1")
WIDE_NARROW = ("wide_0", "wide_1", "narrow_0", "narrow_1")
SECTION_WIDE_NARROW = ("section", "wide_0", "wide_1", "narrow_0", "narrow_1")
MOMENTUM_DECAY = 0.9
STEP_RATE = 0.01


def over_axes(shard, axes):
    for axis in axes:
        shard = lax.psum(shard, axis)
    return shard


def on_device(
    normed_inputs,
    value_cotangent,
    expert_hidden,
    expert_cotangent,
    slot_gate,
    slot_count,
    expert_weight,
    expert_moment,
    value_weight,
    value_moment,
):
    input_rows = normed_inputs[0, 0].reshape(-1, normed_inputs.shape[-1])
    value_cot_rows = value_cotangent[0, 0].reshape(-1, value_cotangent.shape[-1])
    hidden_local = expert_hidden[0, 0]
    cotangent = expert_cotangent[0, 0]
    gate_local = slot_gate[0, 0]
    live_count = slot_count[0, 0]
    cot_piece = lax.all_gather(cotangent, WIDE, axis=1, tiled=True)
    gate_piece = lax.all_gather(gate_local, WIDE, axis=1, tiled=True)
    length = cot_piece.shape[1]
    positions = jnp.arange(length, dtype=jnp.int32)
    live = positions[None, :] < live_count[:, None]
    coefficient = jnp.where(
        live, gate_piece.astype(jnp.float32), jnp.zeros(gate_piece.shape, jnp.float32)
    )
    scaled = (coefficient[:, :, None] * cot_piece.astype(jnp.float32)).astype(jnp.bfloat16)
    summed = lax.dot_general(
        hidden_local, scaled, (((0, 1), (0, 1)), ((), ())), preferred_element_type=jnp.float32
    )
    expert_grad = lax.psum_scatter(
        summed.astype(jnp.bfloat16), NARROW, scatter_dimension=1, tiled=True
    ).astype(jnp.float32)
    value_grad = lax.psum_scatter(
        lax.dot_general(
            input_rows, value_cot_rows, (((0,), (0,)), ((), ())), preferred_element_type=jnp.float32
        ).astype(jnp.bfloat16),
        WIDE_NARROW,
        scatter_dimension=0,
        tiled=True,
    ).astype(jnp.float32)
    squares = jnp.sum(expert_grad * expert_grad) + jnp.sum(value_grad * value_grad)
    overall = over_axes(squares, SECTION_WIDE_NARROW)
    entry_count = lax.axis_size("section") * (FF * D + D * KV)
    factor = jnp.minimum(1.0, math.sqrt(entry_count) / jnp.sqrt(overall + 1e-06))
    expert_next = MOMENTUM_DECAY * expert_moment[0] + factor * expert_grad
    value_next = MOMENTUM_DECAY * value_moment[0] + factor * value_grad
    expert_weight_next = (expert_weight[0].astype(jnp.float32) - STEP_RATE * expert_next).astype(
        jnp.bfloat16
    )
    value_weight_next = (value_weight[0].astype(jnp.float32) - STEP_RATE * value_next).astype(
        jnp.bfloat16
    )
    return (expert_weight_next[None], expert_next[None], value_weight_next[None], value_next[None])


def solution(mesh):
    finer = Mesh(
        mesh.devices.reshape(mesh.shape["section"], 4, 2, 2, 2),
        ("section", "wide_0", "wide_1", "narrow_0", "narrow_1"),
    )
    in_specs = (
        P("section", NARROW, None, WIDE, None),
        P("section", NARROW, None, WIDE, None),
        P("section", NARROW, None, None, WIDE),
        P("section", NARROW, None, WIDE, None),
        P("section", NARROW, None, WIDE),
        P("section", NARROW, None),
        P("section", WIDE, NARROW),
        P("section", WIDE, NARROW),
        P("section", WIDE_NARROW, None),
        P("section", WIDE_NARROW, None),
    )
    out_specs = (
        P("section", WIDE, NARROW),
        P("section", WIDE, NARROW),
        P("section", WIDE_NARROW, None),
        P("section", WIDE_NARROW, None),
    )
    return jax.shard_map(
        on_device, mesh=finer, in_specs=in_specs, out_specs=out_specs, check_vma=False
    )
```

profile of v0, /device:TPU:1, one launch (start us, length us, event | category | flops | bytes accessed | tf_op | source)
XLA Modules:
  0.0 304.2 jit_solution(16088000934408733016)
XLA Ops:
  8.1 0.7 all-gather.4.cloned.1.call-update
  8.8 1.1 copy-done
  9.9 7.9 %bitcast_convert_fusion = bf16[4096,1024]{1,0:T(8,128)(2,1)} fusion(bf16[1,1,4,96,4096]{4,3,2,1,0:T(8,128)(2,1)S(1)} %copy-done, bf16[1,1,4,96,1024]{4,3,2,1,0:T(8,128)(2,1)} %param.11), kind=kOutput, calls=%fused_computation.2 | convolution fusion | flops 3225419776 | bytes 12320768 | tf_op jit(solution)/shard_map/dot_general | solution.py:59
  17.8 0.6 copy-done.2
  18.4 0.1 copy.21
  18.6 31.8 %all-gather = bf16[1,1,4,256]{2,1,0,3:T(2,128)(2,1)S(1)} all-gather(bf16[1,1,4,32]{2,1,0,3:T(2,128)(2,1)S(1)} %copy.21), channel_id=2, replica_groups=mesh['section'=4,'wide_0'=4,'wide_1'=2,'narrow_0'=2,'narrow_1'=2] {'wide..., dimensions={3}, use_global_device_ids=true | all-gather | bytes 2304 | tf_op jit(solution)/shard_map/all_gather | solution.py:44
  50.3 0.1 convert_element_type.58
  50.6 70.8 %all-gather.4.cloned.1.call-done = bf16[1,1,4,256,4096]{4,3,2,1,0:T(8,128)(2,1)} async-done(((bf16[1,1,4,32,4096]{4,3,2,1,0:T(8,128)(2,1)}), bf16[1,1,4,256,4096]{4,3,2,1,0:T(8,128)(2,1)}) %all-gather.4.cloned.1.call-update) | async-done | bytes 8388624 | tf_op jit(solution)/shard_map/all_gather | solution.py:43
  121.4 14.1 %fusion.5 = bf16[896,4096]{0,1:T(8,128)(2,1)} fusion(bf16[1,1,4,256,4096]{4,3,2,1,0:T(8,128)(2,1)} %all-gather.4.cloned.1.call-done, f32[4,256]{1,0:T(4,128)S(1)} %copy.22, bf16[1,1,4,256,896]{4,3,2,1,0:T(8,128)(2,1)} %param.12), kind=kOutput, calls=%fused_computation.7 | convolution fusion | flops 7532445696 | bytes 17567744 | tf_op jit(solution)/shard_map/dot_general | solution.py:52
  135.6 17.6 %reduce-scatter.5.cloned.1.call-done = bf16[128,1024]{1,0:T(8,128)(2,1)} async-done(((bf16[4096,1024]{1,0:T(8,128)(2,1)}), bf16[128,1024]{1,0:T(8,128)(2,1)}) %reduce-scatter.5.cloned.1.call-update) | async-done | bytes 262160 | tf_op jit(solution)/shard_map/reduce_scatter | solution.py:58
  153.2 1.7 fusion.16
  154.9 72.7 %reduce-scatter.3.cloned.1.call-done = bf16[896,1024]{0,1:T(8,128)(2,1)} async-done(((bf16[896,4096]{0,1:T(8,128)(2,1)}), bf16[896,1024]{0,1:T(8,128)(2,1)}) %reduce-scatter.3.cloned.1.call-update) | async-done | bytes 1835024 | tf_op jit(solution)/shard_map/reduce_scatter | solution.py:55
  227.6 3.0 %fusion.8 = f32[]{:T(128)} fusion(bf16[896,1024]{0,1:T(8,128)(2,1)} %reduce-scatter.3.cloned.1.call-done), kind=kLoop, calls=%fused_computation.10 | loop fusion | flops 2752511 | bytes 1835012 | tf_op jit(solution)/shard_map/reduce_sum | solution.py:66
  231.9 9.0 %psum.35 = f32[]{:T(128)} all-reduce(f32[]{:T(128)S(6)} %add.26), channel_id=1, replica_groups=mesh['section'=4,'wide_0'=4,'wide_1'=2,'narrow_0'=2,'narrow_1'=2] {'sect..., use_global_device_ids=true, to_apply=%region_4.5 | all-reduce | flops 1 | bytes 8 | tf_op jit(solution)/shard_map/psum | solution.py:21
  240.9 9.3 %psum.36 = f32[]{:T(128)} all-reduce(f32[]{:T(128)} %psum.35), channel_id=1, replica_groups=mesh['section'=4,'wide_0'=4,'wide_1'=2,'narrow_0'=2,'narrow_1'=2] {'wide..., use_global_device_ids=true, to_apply=%region_5.6 | all-reduce | flops 1 | bytes 8 | tf_op jit(solution)/shard_map/psum | solution.py:21
  250.2 5.9 %psum.37 = f32[]{:T(128)} all-reduce(f32[]{:T(128)} %psum.36), channel_id=1, replica_groups=mesh['section'=4,'wide_0'=4,'wide_1'=2,'narrow_0'=2,'narrow_1'=2] {'wide..., use_global_device_ids=true, to_apply=%region_6.7 | all-reduce | flops 1 | bytes 8 | tf_op jit(solution)/shard_map/psum | solution.py:21
  256.0 5.0 %copy.20 = f32[1,896,1024]{1,2,0:T(8,128)} copy(f32[1,896,1024]{2,1,0:T(8,128)} %param.17) | data formatting | bytes 7340032 | tf_op args[7]
  261.1 4.4 %psum.38 = f32[]{:T(128)} all-reduce(f32[]{:T(128)} %psum.37), channel_id=1, replica_groups=mesh['section'=4,'wide_0'=4,'wide_1'=2,'narrow_0'=2,'narrow_1'=2] {'narr..., use_global_device_ids=true, to_apply=%region_7.8 | all-reduce | flops 1 | bytes 8 | tf_op jit(solution)/shard_map/psum | solution.py:21
  265.4 3.8 %copy.19 = bf16[1,896,1024]{1,2,0:T(8,128)(2,1)} copy(bf16[1,896,1024]{2,1,0:T(8,128)(2,1)} %param.16) | data formatting | bytes 3670016 | tf_op args[6]
  269.2 9.4 %psum.39 = f32[]{:T(128)} all-reduce(f32[]{:T(128)} %psum.38), channel_id=1, replica_groups=mesh['section'=4,'wide_0'=4,'wide_1'=2,'narrow_0'=2,'narrow_1'=2] {'narr..., use_global_device_ids=true, to_apply=%region_8.9 | all-reduce | flops 1 | bytes 8 | tf_op jit(solution)/shard_map/psum | solution.py:21
  279.3 6.5 %fusion.12 = (f32[1,896,1024]{1,2,0:T(8,128)}, bf16[1,896,1024]{1,2,0:T(8,128)(2,1)}) fusion(bf16[896,1024]{0,1:T(8,128)(2,1)} %reduce-scatter.3.cloned.1.call-done, f32[1,896,1024]{1,2,0:T(8,128)} %copy.20, f32[]{:T(128)S(6)} %min_shard_map.3, bf16[1,896,1024]{1,2,0:T(8,128)(2,1)} %copy.19), kind=kLoop, calls=%fused_computation.15 | loop fusion | flops 7340032 | bytes 12845060 | tf_op jit(solution)/shard_map/broadcast_in_dim | solution.py:78
  285.8 3.8 %copy.24 = bf16[1,896,1024]{2,1,0:T(8,128)(2,1)} copy(bf16[1,896,1024]{1,2,0:T(8,128)(2,1)} %get-tuple-element.13) | data formatting | bytes 3670016
  289.6 5.0 %copy.25 = f32[1,896,1024]{2,1,0:T(8,128)} copy(f32[1,896,1024]{1,2,0:T(8,128)} %get-tuple-element.12) | data formatting | bytes 7340032
  294.6 2.1 fusion.19
  (13 shorter events, 0.3 us)
Async XLA Ops:
  8.0 1.9 copy-start
  8.0 113.4 %all-gather.4.cloned.1.call-start = ((), (), s32[]{:S(2)}) async-start(), calls=%async_computation.4 | async-start | bytes 9437184 | tf_op jit(solution)/shard_map/all_gather | solution.py:43
  8.7 144.4 %reduce-scatter.5.cloned.1.call-start = ((), (), s32[]{:S(2)}) async-start(), calls=%async_computation.3 | async-start | bytes 8650752 | tf_op jit(solution)/shard_map/reduce_scatter | solution.py:58
  17.8 0.7 copy-start.2
  17.8 32.7 %copy-start.3 = (s32[1,1,4]{2,1,0:T(1,128)S(1)}, s32[1,1,4]{2,1,0:T(1,128)}, u32[]{:S(2)}) copy-start(s32[1,1,4]{2,1,0:T(1,128)} %param.15) | copy-start | bytes 52
  17.8 209.8 %reduce-scatter.3.cloned.1.call-start = ((), (), s32[]{:S(2)}) async-start(), calls=%async_computation.2 | async-start | bytes 9175040 | tf_op jit(solution)/shard_map/reduce_scatter | solution.py:55
  289.6 5.0 %copy-start.1 = (bf16[128,1024]{1,0:T(8,128)(2,1)S(1)}, bf16[128,1024]{1,0:T(8,128)(2,1)}, u32[]{:S(2)}) copy-start(bf16[128,1024]{1,0:T(8,128)(2,1)} %reduce-scatter.5.cloned.1.call-done) | copy-start | bytes 786436
Sparse Core Ops, SparseCore 0:
  11.1 110.2 all-gather.3
Sparse Core Ops, SparseCore 1:
  17.9 135.2 reduce-scatter.4
  155.4 72.1 reduce-scatter.2
where the time goes:
time: 305 us; the launch traced here: 304 us
  waiting for transfers between devices  162 us (53%)
  blocking collectives  69.7 us (23%)
  matrix products  22 us (7%)
  local copies, waits for them, and re-layouts  19.5 us (6%)
  between operations  17.5 us (6%)
  other arithmetic  13.5 us (4%)
    reduce_scatter x1, waiting for transfers between devices, on_device(): lax.psum_scatter(summed.astype(jnp.bfloat16), NARROW, scatter_dimension=1...  72.7 us
    all_gather x1, waiting for transfers between devices, on_device(): cot_piece = lax.all_gather(cotangent, WIDE, axis=1, tiled=True)  70.8 us
    psum x5, blocking collectives, over_axes(): shard = lax.psum(shard, axis)  37.9 us
    all_gather x1, blocking collectives, on_device(): gate_piece = lax.all_gather(gate_local, WIDE, axis=1, tiled=True)  31.8 us
    unnamed x13, local copies, waits for them, and re-layouts  19.4 us
    reduce_scatter x1, waiting for transfers between devices, on_device(): lax.psum_scatter(lax.dot_general(input_rows, value_cot_rows, (((0,), (0,)...  17.6 us
    dot_general x1, matrix products, on_device(): lax.dot_general(hidden_local, scaled, (((0, 1), (0, 1)), ((), ())), prefe...  14.1 us
    dot_general x1, matrix products, on_device(): lax.dot_general(input_rows, value_cot_rows, (((0,), (0,)), ((), ())), pre...  7.87 us
  transfers between devices with their start and end apart: 3, of which 3 were waited for; matrix products, arithmetic and copies ran while one was open for 8% of the time, Pallas kernels for 0%

commit v1 on v0

--- a/solution.py
+++ b/solution.py
@@ -41,7 +41,9 @@
     gate_local = slot_gate[0, 0]
     live_count = slot_count[0, 0]
     cot_piece = lax.all_gather(cotangent, WIDE, axis=1, tiled=True)
-    gate_piece = lax.all_gather(gate_local, WIDE, axis=1, tiled=True)
+    gate_piece = jnp.concatenate(
+        lax.all_to_all(jnp.stack([gate_local] * lax.axis_size(WIDE)), WIDE, 0, 0), axis=1
+    )
     length = cot_piece.shape[1]
     positions = jnp.arange(length, dtype=jnp.int32)
     live = positions[None, :] < live_count[:, None]

time: 305 us -> 304 us (level)
  blocking collectives: 69.7 us -> 52.6 us
  waiting for transfers between devices: 162 us -> 178 us
    all_gather x1 -> x0, blocking collectives: 31.8 us -> none  [on_device(): gate_piece = lax.all_gather(gate_local, WIDE, axis=1, tiled=True)]
    all_gather x1, waiting for transfers between devices: 70.8 us -> 86.8 us  [on_device(): cot_piece = lax.all_gather(cotangent, WIDE, axis=1, tiled=True)]
    all_to_all x0 -> x1, blocking collectives: none -> 14.7 us  [on_device(): lax.all_to_all(jnp.stack([gate_local] * lax.axis_size(WIDE)), WIDE, 0, 0)]
    unnamed x13 -> x12, local copies, waits for them, and re-layouts: 19.4 us -> 19.3 us
where the time goes in v1:
time: 304 us; the launch traced here: 303 us
  waiting for transfers between devices  178 us (59%)
  blocking collectives  52.6 us (17%)
  matrix products  22 us (7%)
  local copies, waits for them, and re-layouts  19.4 us (6%)
  between operations  17.5 us (6%)
  other arithmetic  13.4 us (4%)
    all_gather x1, waiting for transfers between devices, on_device(): cot_piece = lax.all_gather(cotangent, WIDE, axis=1, tiled=True)  86.8 us
    reduce_scatter x1, waiting for transfers between devices, on_device(): lax.psum_scatter(summed.astype(jnp.bfloat16), NARROW, scatter_dimension=1...  72.7 us
    psum x5, blocking collectives, over_axes(): shard = lax.psum(shard, axis)  37.9 us
    unnamed x12, local copies, waits for them, and re-layouts  19.3 us
    reduce_scatter x1, waiting for transfers between devices, on_device(): lax.psum_scatter(lax.dot_general(input_rows, value_cot_rows, (((0,), (0,)...  17.6 us
    all_to_all x1, blocking collectives, on_device(): lax.all_to_all(jnp.stack([gate_local] * lax.axis_size(WIDE)), WIDE, 0, 0)  14.7 us
    dot_general x1, matrix products, on_device(): lax.dot_general(hidden_local, scaled, (((0, 1), (0, 1)), ((), ())), prefe...  14.1 us
    dot_general x1, matrix products, on_device(): lax.dot_general(input_rows, value_cot_rows, (((0,), (0,)), ((), ())), pre...  7.87 us
  transfers between devices with their start and end apart: 3, of which 3 were waited for; matrix products, arithmetic and copies ran while one was open for 8% of the time, Pallas kernels for 0%

profile of v1, /device:TPU:1, one launch (start us, length us, event | category | flops | bytes accessed | tf_op | source)
XLA Modules:
  0.0 302.8 jit_solution(6363602383829753946)
XLA Ops:
  8.1 0.7 all-gather.3.cloned.1.call-update
  8.8 1.1 copy-done
  9.9 7.9 %bitcast_convert_fusion = bf16[4096,1024]{1,0:T(8,128)(2,1)} fusion(bf16[1,1,4,96,4096]{4,3,2,1,0:T(8,128)(2,1)S(1)} %copy-done, bf16[1,1,4,96,1024]{4,3,2,1,0:T(8,128)(2,1)} %param.11), kind=kOutput, calls=%fused_computation.2 | convolution fusion | flops 3225419776 | bytes 12320768 | tf_op jit(solution)/shard_map/dot_general | solution.py:61
  17.8 0.6 copy-done.2
  18.4 14.7 %all_to_all.5 = bf16[8,4,32]{2,1,0:T(4,128)(2,1)S(1)} all-to-all(bf16[8,4,32]{2,1,0:T(4,128)(2,1)S(1)} %stack.3), channel_id=1, replica_groups=mesh['section'=4,'wide_0'=4,'wide_1'=2,'narrow_0'=2,'narrow_1'=2] {'wide..., dimensions={0} | all-to-all | bytes 4096 | tf_op jit(solution)/shard_map/all_to_all | solution.py:45
  33.2 0.1 reshape.61
  33.3 0.1 fusion.21
  33.4 86.8 %all-gather.3.cloned.1.call-done = bf16[1,1,4,256,4096]{4,3,2,1,0:T(8,128)(2,1)} async-done(((bf16[1,1,4,32,4096]{4,3,2,1,0:T(8,128)(2,1)}), bf16[1,1,4,256,4096]{4,3,2,1,0:T(8,128)(2,1)}) %all-gather.3.cloned.1.call-update) | async-done | bytes 8388624 | tf_op jit(solution)/shard_map/all_gather | solution.py:43
  120.1 14.1 %fusion.5 = bf16[896,4096]{0,1:T(8,128)(2,1)} fusion(bf16[1,1,4,256,4096]{4,3,2,1,0:T(8,128)(2,1)} %all-gather.3.cloned.1.call-done, f32[4,256]{1,0:T(4,128)S(1)} %fusion.21, bf16[1,1,4,256,896]{4,3,2,1,0:T(8,128)(2,1)} %param.12), kind=kOutput, calls=%fused_computation.7 | convolution fusion | flops 7532445696 | bytes 17567744 | tf_op jit(solution)/shard_map/dot_general | solution.py:54
  134.3 17.6 %reduce-scatter.5.cloned.1.call-done = bf16[128,1024]{1,0:T(8,128)(2,1)} async-done(((bf16[4096,1024]{1,0:T(8,128)(2,1)}), bf16[128,1024]{1,0:T(8,128)(2,1)}) %reduce-scatter.5.cloned.1.call-update) | async-done | bytes 262160 | tf_op jit(solution)/shard_map/reduce_scatter | solution.py:60
  151.9 1.7 fusion.16
  153.5 72.7 %reduce-scatter.3.cloned.1.call-done = bf16[896,1024]{0,1:T(8,128)(2,1)} async-done(((bf16[896,4096]{0,1:T(8,128)(2,1)}), bf16[896,1024]{0,1:T(8,128)(2,1)}) %reduce-scatter.3.cloned.1.call-update) | async-done | bytes 1835024 | tf_op jit(solution)/shard_map/reduce_scatter | solution.py:57
  226.3 3.0 %fusion.8 = f32[]{:T(128)} fusion(bf16[896,1024]{0,1:T(8,128)(2,1)} %reduce-scatter.3.cloned.1.call-done), kind=kLoop, calls=%fused_computation.10 | loop fusion | flops 2752511 | bytes 1835012 | tf_op jit(solution)/shard_map/reduce_sum | solution.py:68
  230.6 9.0 %psum.35 = f32[]{:T(128)} all-reduce(f32[]{:T(128)S(6)} %add.26), channel_id=1, replica_groups=mesh['section'=4,'wide_0'=4,'wide_1'=2,'narrow_0'=2,'narrow_1'=2] {'sect..., use_global_device_ids=true, to_apply=%region_4.5 | all-reduce | flops 1 | bytes 8 | tf_op jit(solution)/shard_map/psum | solution.py:21
  239.6 9.3 %psum.36 = f32[]{:T(128)} all-reduce(f32[]{:T(128)} %psum.35), channel_id=1, replica_groups=mesh['section'=4,'wide_0'=4,'wide_1'=2,'narrow_0'=2,'narrow_1'=2] {'wide..., use_global_device_ids=true, to_apply=%region_5.6 | all-reduce | flops 1 | bytes 8 | tf_op jit(solution)/shard_map/psum | solution.py:21
  248.8 5.9 %psum.37 = f32[]{:T(128)} all-reduce(f32[]{:T(128)} %psum.36), channel_id=1, replica_groups=mesh['section'=4,'wide_0'=4,'wide_1'=2,'narrow_0'=2,'narrow_1'=2] {'wide..., use_global_device_ids=true, to_apply=%region_6.7 | all-reduce | flops 1 | bytes 8 | tf_op jit(solution)/shard_map/psum | solution.py:21
  254.7 5.0 %copy.25 = f32[1,896,1024]{1,2,0:T(8,128)} copy(f32[1,896,1024]{2,1,0:T(8,128)} %param.17) | data formatting | bytes 7340032 | tf_op args[7]
  259.7 4.4 %psum.38 = f32[]{:T(128)} all-reduce(f32[]{:T(128)} %psum.37), channel_id=1, replica_groups=mesh['section'=4,'wide_0'=4,'wide_1'=2,'narrow_0'=2,'narrow_1'=2] {'narr..., use_global_device_ids=true, to_apply=%region_7.8 | all-reduce | flops 1 | bytes 8 | tf_op jit(solution)/shard_map/psum | solution.py:21
  264.1 3.8 %copy.24 = bf16[1,896,1024]{1,2,0:T(8,128)(2,1)} copy(bf16[1,896,1024]{2,1,0:T(8,128)(2,1)} %param.16) | data formatting | bytes 3670016 | tf_op args[6]
  267.9 9.4 %psum.39 = f32[]{:T(128)} all-reduce(f32[]{:T(128)} %psum.38), channel_id=1, replica_groups=mesh['section'=4,'wide_0'=4,'wide_1'=2,'narrow_0'=2,'narrow_1'=2] {'narr..., use_global_device_ids=true, to_apply=%region_8.9 | all-reduce | flops 1 | bytes 8 | tf_op jit(solution)/shard_map/psum | solution.py:21
  278.0 6.5 %fusion.12 = (f32[1,896,1024]{1,2,0:T(8,128)}, bf16[1,896,1024]{1,2,0:T(8,128)(2,1)}) fusion(bf16[896,1024]{0,1:T(8,128)(2,1)} %reduce-scatter.3.cloned.1.call-done, f32[1,896,1024]{1,2,0:T(8,128)} %copy.25, f32[]{:T(128)S(6)} %min_shard_map.3, bf16[1,896,1024]{1,2,0:T(8,128)(2,1)} %copy.24), kind=kLoop, calls=%fused_computation.15 | loop fusion | flops 7340032 | bytes 12845060 | tf_op jit(solution)/shard_map/broadcast_in_dim | solution.py:80
  284.5 3.8 %copy.28 = bf16[1,896,1024]{2,1,0:T(8,128)(2,1)} copy(bf16[1,896,1024]{1,2,0:T(8,128)(2,1)} %get-tuple-element.17) | data formatting | bytes 3670016
  288.3 5.0 %copy.29 = f32[1,896,1024]{2,1,0:T(8,128)} copy(f32[1,896,1024]{1,2,0:T(8,128)} %get-tuple-element.16) | data formatting | bytes 7340032
  293.3 2.1 fusion.19
  (14 shorter events, 0.2 us)
Async XLA Ops:
  8.0 1.9 copy-start
  8.0 112.1 %all-gather.3.cloned.1.call-start = ((), (), s32[]{:S(2)}) async-start(), calls=%async_computation.5 | async-start | bytes 9437184 | tf_op jit(solution)/shard_map/all_gather | solution.py:43
  8.7 143.1 %reduce-scatter.5.cloned.1.call-start = ((), (), s32[]{:S(2)}) async-start(), calls=%async_computation.4 | async-start | bytes 8650752 | tf_op jit(solution)/shard_map/reduce_scatter | solution.py:60
  17.8 0.7 copy-start.2
  17.8 15.5 %copy-start.3 = (s32[1,1,4]{2,1,0:T(1,128)S(1)}, s32[1,1,4]{2,1,0:T(1,128)}, u32[]{:S(2)}) copy-start(s32[1,1,4]{2,1,0:T(1,128)} %param.15) | copy-start | bytes 52
  17.8 208.5 %reduce-scatter.3.cloned.1.call-start = ((), (), s32[]{:S(2)}) async-start(), calls=%async_computation.3 | async-start | bytes 9175040 | tf_op jit(solution)/shard_map/reduce_scatter | solution.py:57
  288.3 5.0 %copy-start.1 = (bf16[128,1024]{1,0:T(8,128)(2,1)S(1)}, bf16[128,1024]{1,0:T(8,128)(2,1)}, u32[]{:S(2)}) copy-start(bf16[128,1024]{1,0:T(8,128)(2,1)} %reduce-scatter.5.cloned.1.call-done) | copy-start | bytes 786436
Sparse Core Ops, SparseCore 0:
  11.1 108.9 all-gather.2
Sparse Core Ops, SparseCore 1:
  17.9 133.9 reduce-scatter.4
  154.1 72.1 reduce-scatter.2
